TPU v7x, 32 devices: a whole 2x2x4 slice. The times are simulated.
32 devices in a mesh: groups: 2 (over x), seq: 16 (over z, y, core).
Axes of the slice: x: 2, y: 2, z: 4, core: 2. Of those that a mesh axis runs over, the one named last changes fastest.
Arguments:
- queries: bfloat16 [4096, 1792], P(('groups', 'seq')), parts along dimension 0, may hold values from -100 to 100
- key_rows: bfloat16 [4096, 256], P(('groups', 'seq')), parts along dimension 0, may hold values from -100 to 100
- value_rows: bfloat16 [4096, 256], P(('groups', 'seq')), parts along dimension 0, may hold values from -6 to 6
- span_order: int32 [64], P('groups'), parts along dimension 0, may hold values from 0 to 31, each once
- kept_blocks: int32 [4, 1], P('groups'), parts along dimension 0, may hold values from 0 to 3, as said below
Outputs:
- attended: bfloat16 [4096, 1792], P(('groups', 'seq')), parts along dimension 0
- kept_cache: bfloat16 [1024, 512], P(('groups', 'seq')), parts along dimension 0
There are 2 independent parts, one for each index of `groups`. A program takes and returns all parts, laid end to end along the dimension named above; each array names one. Nothing has to cross between parts.
Inputs may be any that keep to these rules, and one draw needn't show every extreme that they name: `kept_blocks`: each row lists 1 different blocks.
All inputs are finite; a program needn't handle non-finite values.
Results may differ from a plain program's by a relative error of at most 0.0055.
Values may be sent and summed in bfloat16 or wider, within the bound.
A program may use at most 64 MiB of HBM per device.

v0:
```python
import math
import jax
import jax.numpy as jnp
from jax import lax
from jax.sharding import PartitionSpec as P

HEAD_DIM = 128
BLOCK = 512


def token_positions(span_order, span_len):
    within = jnp.arange(span_len, dtype=jnp.int32)
    return (span_order[:, None] * span_len + within[None, :]).reshape(-1)


def cache_sources(kept_blocks, row_ids):
    block_ids = row_ids // BLOCK
    match = (
        jnp.arange(kept_blocks.shape[1], dtype=jnp.int32)[None, None, :] == block_ids[None, :, None]
    )
    chosen = jnp.sum(jnp.where(match, kept_blocks[:, None, :], 0), axis=-1)
    return chosen * BLOCK + row_ids[None, :] % BLOCK


def local(queries, key_rows, value_rows, span_order, kept_blocks):
    seq_count = lax.axis_size("seq")
    my_index = lax.axis_index("seq")
    query_rows = queries.shape[0]
    kv_heads = key_rows.shape[1] // HEAD_DIM
    group_size = queries.shape[1] // key_rows.shape[1]
    scale = 1.0 / math.sqrt(HEAD_DIM)
    positions = token_positions(span_order, query_rows // 2)
    query_pos = lax.dynamic_slice_in_dim(positions, my_index * query_rows, query_rows)
    query_heads = queries.reshape(query_rows, kv_heads, group_size, HEAD_DIM)
    cache_local = kept_blocks.shape[1] * BLOCK // seq_count
    cache_src = cache_sources(
        kept_blocks, my_index * cache_local + jnp.arange(cache_local, dtype=jnp.int32)
    )

    def pick_rows(sources, key_part, value_part, part_pos):
        onehot = (sources[:, :, None] == part_pos[None, None, :]).astype(jnp.bfloat16)
        count = key_part.shape[0]
        out_rows = sources.shape[1]
        picked_keys = jnp.einsum(
            "hrk,khd->rhd",
            onehot,
            key_part.reshape(count, kv_heads, HEAD_DIM),
            preferred_element_type=jnp.float32,
        )
        picked_values = jnp.einsum(
            "hrk,khd->rhd",
            onehot,
            value_part.reshape(count, kv_heads, HEAD_DIM),
            preferred_element_type=jnp.float32,
        )
        return jnp.concatenate(
            [picked_keys.reshape(out_rows, -1), picked_values.reshape(out_rows, -1)], axis=1
        )

    def attend_block(state, block_keys, block_values, block_pos):
        running_max, totals, accum = (state[0], state[1], state[2])
        count = block_keys.shape[0]
        scores = (
            jnp.einsum(
                "qhgd,khd->hgqk",
                query_heads,
                block_keys.reshape(count, kv_heads, HEAD_DIM),
                preferred_element_type=jnp.float32,
            )
            * scale
        )
        visible = block_pos[None, None, None, :] <= query_pos[None, None, :, None]
        scores = jnp.where(visible, scores, -1e30)
        new_max = jnp.maximum(running_max, jnp.max(scores, axis=-1))
        weights = jnp.where(visible, jnp.exp(scores - new_max[..., None]), 0.0)
        factor = jnp.exp(running_max - new_max)
        totals = totals * factor + jnp.sum(weights, axis=-1)
        mixed = jnp.einsum(
            "hgqk,khd->hgqd",
            weights.astype(jnp.bfloat16),
            block_values.reshape(count, kv_heads, HEAD_DIM),
            preferred_element_type=jnp.float32,
        )
        accum = accum * factor[..., None] + mixed
        return (new_max, totals, accum)

    initial = (
        jnp.full((kv_heads, group_size, query_rows), -1e30, jnp.float32),
        jnp.zeros((kv_heads, group_size, query_rows), jnp.float32),
        jnp.zeros((kv_heads, group_size, query_rows, HEAD_DIM), jnp.float32),
    )
    initial = initial + (jnp.zeros((cache_local, 2 * kv_heads * HEAD_DIM), jnp.float32),)
    piece_keys = lax.all_gather(key_rows, "seq", axis=0, tiled=True)
    piece_values = lax.all_gather(value_rows, "seq", axis=0, tiled=True)
    count = piece_keys.shape[0]
    width = math.gcd(count, 512)

    def inner(step_index, inner_state):
        offset = (step_index * width).astype(jnp.int32)
        block_keys = lax.dynamic_slice_in_dim(piece_keys, offset, width, 0)
        block_values = lax.dynamic_slice_in_dim(piece_values, offset, width, 0)
        block_pos = lax.dynamic_slice_in_dim(positions, offset, width)
        updated = attend_block(inner_state, block_keys, block_values, block_pos)
        extra = (inner_state[3] + pick_rows(cache_src, block_keys, block_values, block_pos),)
        return updated + extra

    final = lax.fori_loop(0, count // width, inner, initial)
    attended = final[2] / final[1][..., None]
    attended = jnp.transpose(attended, (2, 0, 1, 3)).reshape(query_rows, -1).astype(jnp.bfloat16)
    kept_cache = final[3].astype(jnp.bfloat16)
    return (attended, kept_cache)


def solution(mesh):
    placed = (
        P(("groups", "seq"), None),
        P(("groups", "seq"), None),
        P(("groups", "seq"), None),
        P("groups"),
        P("groups", None),
    )
    return jax.shard_map(
        local,
        mesh=mesh,
        in_specs=placed,
        out_specs=(P(("groups", "seq"), None), P(("groups", "seq"), None)),
        check_vma=False,
    )
```

profile of v0, /device:TPU:0, one launch (start us, length us, event | category | flops | bytes accessed | tf_op | source)
XLA Modules:
  0.0 120.7 jit_solution(2158012903326060525)
XLA Ops:
  7.2 1.6 %copy.16 = bf16[128,256]{0,1:T(8,128)(2,1)} copy(bf16[128,256]{1,0:T(8,128)(2,1)} %param.8) | data formatting | bytes 131072 | tf_op args[1]
  8.9 1.6 %copy.18 = bf16[128,256]{0,1:T(8,128)(2,1)} copy(bf16[128,256]{1,0:T(8,128)(2,1)} %param.9) | data formatting | bytes 131072 | tf_op args[2]
  10.5 0.7 broadcast_multiply_fusion
  11.3 1.3 %copy.17 = bf16[128,1792]{0,1:T(8,128)(2,1)S(1)} copy(bf16[128,1792]{1,0:T(8,128)(2,1)} %param.7) | data formatting | bytes 917504 | tf_op args[0]
  12.6 0.3 copy.19
  13.0 37.1 %all-gather.3.cloned.1.call-done = bf16[2048,256]{0,1:T(8,128)(2,1)} async-done(((bf16[128,256]{0,1:T(8,128)(2,1)}), bf16[2048,256]{0,1:T(8,128)(2,1)}) %all-gather.3.cloned.1.call-update) | async-done | bytes 1048592 | tf_op jit(solution)/shard_map/all_gather | solution.py:93
  50.1 38.4 %all-gather.5.cloned.1.call-done = bf16[2048,256]{0,1:T(8,128)(2,1)} async-done(((bf16[128,256]{0,1:T(8,128)(2,1)}), bf16[2048,256]{0,1:T(8,128)(2,1)}) %all-gather.5.cloned.1.call-update) | async-done | bytes 1048592 | tf_op jit(solution)/shard_map/all_gather | solution.py:94
  88.5 23.3 %while.20 = (s32[]{:T(128)}, f32[2,7,128]{2,1,0:T(8,128)S(1)}, f32[2,7,128]{2,1,0:T(8,128)S(1)}, f32[2,7,128,128]{3,2,1,0:T(8,128)S(1)}, f32[32,512]{1,0:T(8,128...) while((s32[]{:T(128)}, f32[2,7,128]{2,1,0:T(8,128)S(1)}, ...), condition=%wide.region_3.4_spmd.clone, body=%wide.region_0.3_spmd.clone.sunk | while | flops 499344320 | bytes 16182928 | solution.py:107
  88.5 0.7 multiply_add_fusion.2
  89.5 1.1 constant_dynamic-slice_fusion.3
  90.8 0.2 convolution_bitcast_fusion.5
  91.1 0.8 fusion.47
  91.9 0.9 fusion.48
  92.8 1.5 %fusion.50 = f32[2,7,128,128]{3,2,1,0:T(8,128)S(1)} fusion(bf16[512,2,128,1]{0,2,3,1:T(8,128)(2,1)S(1)} %bitcast.80, f32[2,512,128,7]{2,1,3,0:T(8,128)S(1)} %get-tuple-element.372, f32[2,7,128]{2,1,0:T(8,128)S(1)} %select_maximum_fusion.2, pred[128,512]{0,1:T(8,128)(4,1)S(1)} %broadcast_compare_fusion.2, ...), kind=kOutput, calls=%fused_computation.8.clone.1 | convolution fusion | flops 240156672 | bytes 5847041 | tf_op jit(solution)/shard_map/while/body/eval_jaxpr/hgqk,khd->hgqd/dot_general | solution.py:78
  94.4 0.7 multiply_add_fusion.2
  95.3 1.1 constant_dynamic-slice_fusion.3
  96.9 0.8 fusion.47
  97.7 0.9 fusion.48
  98.6 1.5 %fusion.50 = f32[2,7,128,128]{3,2,1,0:T(8,128)S(1)} fusion(bf16[512,2,128,1]{0,2,3,1:T(8,128)(2,1)S(1)} %bitcast.80, f32[2,512,128,7]{2,1,3,0:T(8,128)S(1)} %get-tuple-element.372, f32[2,7,128]{2,1,0:T(8,128)S(1)} %select_maximum_fusion.2, pred[128,512]{0,1:T(8,128)(4,1)S(1)} %broadcast_compare_fusion.2, ...), kind=kOutput, calls=%fused_computation.8.clone.1 | convolution fusion | flops 240156672 | bytes 5847041 | tf_op jit(solution)/shard_map/while/body/eval_jaxpr/hgqk,khd->hgqd/dot_general | solution.py:78
  100.2 0.7 multiply_add_fusion.2
  101.1 1.1 constant_dynamic-slice_fusion.3
  102.7 0.8 fusion.47
  103.5 0.9 fusion.48
  104.4 1.5 %fusion.50 = f32[2,7,128,128]{3,2,1,0:T(8,128)S(1)} fusion(bf16[512,2,128,1]{0,2,3,1:T(8,128)(2,1)S(1)} %bitcast.80, f32[2,512,128,7]{2,1,3,0:T(8,128)S(1)} %get-tuple-element.372, f32[2,7,128]{2,1,0:T(8,128)S(1)} %select_maximum_fusion.2, pred[128,512]{0,1:T(8,128)(4,1)S(1)} %broadcast_compare_fusion.2, ...), kind=kOutput, calls=%fused_computation.8.clone.1 | convolution fusion | flops 240156672 | bytes 5847041 | tf_op jit(solution)/shard_map/while/body/eval_jaxpr/hgqk,khd->hgqd/dot_general | solution.py:78
  106.0 0.7 multiply_add_fusion.2
  106.9 1.1 constant_dynamic-slice_fusion.3
  108.5 0.8 fusion.47
  109.3 0.9 fusion.48
  110.2 1.5 %fusion.50 = f32[2,7,128,128]{3,2,1,0:T(8,128)S(1)} fusion(bf16[512,2,128,1]{0,2,3,1:T(8,128)(2,1)S(1)} %bitcast.80, f32[2,512,128,7]{2,1,3,0:T(8,128)S(1)} %get-tuple-element.372, f32[2,7,128]{2,1,0:T(8,128)S(1)} %select_maximum_fusion.2, pred[128,512]{0,1:T(8,128)(4,1)S(1)} %broadcast_compare_fusion.2, ...), kind=kOutput, calls=%fused_computation.8.clone.1 | convolution fusion | flops 240156672 | bytes 5847041 | tf_op jit(solution)/shard_map/while/body/eval_jaxpr/hgqk,khd->hgqd/dot_general | solution.py:78
  111.8 0.3 copy.20
  112.2 1.0 copy.21
  113.2 0.6 convert_element_type.25
  (53 shorter events, 3.1 us)
Async XLA Ops:
  7.2 42.9 %all-gather.3.cloned.1.call-start = ((), (), s32[]{:S(2)}) async-start(), calls=%async_computation | async-start | bytes 1114112 | tf_op jit(solution)/shard_map/all_gather | solution.py:93
  8.8 79.7 %all-gather.5.cloned.1.call-start = ((), (), s32[]{:S(2)}) async-start(), calls=%async_computation.1 | async-start | bytes 1114112 | tf_op jit(solution)/shard_map/all_gather | solution.py:94
Sparse Core Ops, SparseCore 0:
  10.7 39.3 all-gather.2
  52.3 36.2 all-gather.4
where the time goes:
time: 121 us
  waiting for transfers between devices  75.6 us (62%)
  between operations  14.1 us (12%)
  matrix products  11 us (9%)
  local copies, waits for them, and re-layouts  10.8 us (9%)
  other arithmetic  8.65 us (7%)
    all_gather x1, waiting for transfers between devices, local(): piece_values = lax.all_gather(value_rows, 'seq', axis=0, tiled=True)  38.4 us
    all_gather x1, waiting for transfers between devices, local(): piece_keys = lax.all_gather(key_rows, 'seq', axis=0, tiled=True)  37.1 us
    dot_general x4, matrix products, attend_block(): jnp.einsum('hgqk,khd->hgqd', weights.astype(jnp.bfloat16), block_values.r...  6.16 us
    unnamed x5, local copies, waits for them, and re-layouts  5.68 us
    dynamic_slice x4, local copies, waits for them, and re-layouts, inner(): block_values = lax.dynamic_slice_in_dim(piece_values, offset, width, 0)  4.29 us
    reduce_sum x4, other arithmetic, attend_block(): totals = totals * factor + jnp.sum(weights, axis=-1)  3.54 us
    dot_general x4, matrix products, attend_block(): jnp.einsum('qhgd,khd->hgqk', query_heads, block_keys.reshape(count, kv_he...  3.13 us
    add x4, other arithmetic, cache_sources(): return chosen * BLOCK + row_ids[None, :] % BLOCK  2.91 us
  transfers between devices with their start and end apart: 2, of which 2 were waited for; matrix products, arithmetic and copies ran while one was open for 3% of the time, Pallas kernels for 0%

commit v1 on v0

--- a/solution.py
+++ b/solution.py
@@ -1,3 +1,4 @@
+import functools
 import math
 import jax
 import jax.numpy as jnp
@@ -6,6 +7,22 @@
 
 HEAD_DIM = 128
 BLOCK = 512
+
+
+def solve_packet_on_mesh(v0, shard_axis):
+    shares = jax.lax.axis_size(shard_axis)
+    y2 = [(idx - 1, idx) for idx in range(1, shares)] + [(shares - 1, 0)]
+    m_next = v0
+    grid = [m_next]
+    for _ in tuple(range(shares - 1)):
+        m_next = jax.lax.ppermute(m_next, shard_axis, y2)
+        grid += [m_next]
+    carry = jnp.concatenate([*reversed(grid)], axis=0)
+    f_now = jax.lax.axis_index(shard_axis)
+    return jnp.roll(carry, (f_now + 1) * m_next.shape[0], axis=0)
+
+
+meet_row = functools.partial(solve_packet_on_mesh, shard_axis="seq")
 
 
 def token_positions(span_order, span_len):
@@ -91,7 +108,7 @@
     )
     initial = initial + (jnp.zeros((cache_local, 2 * kv_heads * HEAD_DIM), jnp.float32),)
     piece_keys = lax.all_gather(key_rows, "seq", axis=0, tiled=True)
-    piece_values = lax.all_gather(value_rows, "seq", axis=0, tiled=True)
+    piece_values = meet_row(value_rows)
     count = piece_keys.shape[0]
     width = math.gcd(count, 512)
 

time: 121 us -> 143 us (1.18)
  waiting for transfers between devices: 75.6 us -> 99.8 us
  other arithmetic: 8.65 us -> 6.02 us
    ppermute x0 -> x15, waiting for transfers between devices: none -> 92.5 us  [solve_packet_on_mesh(): m_next = jax.lax.ppermute(m_next, shard_axis, y2)]
    all_gather x1 -> x0, waiting for transfers between devices: 38.4 us -> none  [local(): piece_values = lax.all_gather(value_rows, 'seq', axis=0, tiled=True)]
    all_gather x1, waiting for transfers between devices: 37.1 us -> 7.25 us  [local(): piece_keys = lax.all_gather(key_rows, 'seq', axis=0, tiled=True)]
    add x4, other arithmetic: 2.91 us -> 0.29 us  [cache_sources(): return chosen * BLOCK + row_ids[None, :] % BLOCK]
    unnamed x5 -> x38, local copies, waits for them, and re-layouts: 5.68 us -> 5.66 us
  transfers between devices with their start and end apart: 2 -> 16, of which waited for: 2 -> 16; matrix products, arithmetic and copies ran while one was open for 3% -> 3% of each run, Pallas kernels for 0% -> 0%
where the time goes in v1:
time: 143 us
  waiting for transfers between devices  99.8 us (70%)
  between operations  14.3 us (10%)
  matrix products  11 us (8%)
  local copies, waits for them, and re-layouts  10.6 us (7%)
  other arithmetic  6.02 us (4%)
    ppermute x15, waiting for transfers between devices, solve_packet_on_mesh(): m_next = jax.lax.ppermute(m_next, shard_axis, y2)  92.5 us
    all_gather x1, waiting for transfers between devices, local(): piece_keys = lax.all_gather(key_rows, 'seq', axis=0, tiled=True)  7.25 us
    dot_general x4, matrix products, attend_block(): jnp.einsum('hgqk,khd->hgqd', weights.astype(jnp.bfloat16), block_values.r...  6.16 us
    unnamed x38, local copies, waits for them, and re-layouts  5.66 us
    dynamic_slice x4, local copies, waits for them, and re-layouts, inner(): block_values = lax.dynamic_slice_in_dim(piece_values, offset, width, 0)  4 us
    reduce_sum x4, other arithmetic, attend_block(): totals = totals * factor + jnp.sum(weights, axis=-1)  3.54 us
    dot_general x4, matrix products, attend_block(): jnp.einsum('qhgd,khd->hgqk', query_heads, block_keys.reshape(count, kv_he...  3.13 us
  transfers between devices with their start and end apart: 16, of which 16 were waited for; matrix products, arithmetic and copies ran while one was open for 3% of the time, Pallas kernels for 0%

profile of v1, /device:TPU:0, one launch (start us, length us, event | category | flops | bytes accessed | tf_op | source)
XLA Modules:
  0.0 142.8 jit_solution(8859586658509027111)
XLA Ops:
  7.2 0.9 copy.18
  8.7 6.9 %collective-permute-done = bf16[128,256]{0,1:T(8,128)(2,1)S(1)} collective-permute-done((bf16[128,256]{0,1:T(8,128)(2,1)S(1)}, bf16[128,256]{0,1:T(8,128)(2,1)S(1)}, u32[]{:S(2)}, u32[]{:S(2)}) %collective-permute-start) | collective-permute-done | bytes 65568 | tf_op jit(solution)/shard_map/ppermute | solution.py:18
  15.6 6.4 %collective-permute-done.1 = bf16[128,256]{0,1:T(8,128)(2,1)S(1)} collective-permute-done((bf16[128,256]{0,1:T(8,128)(2,1)S(1)}, bf16[128,256]{0,1:T(8,128)(2,1)S(1)}, u32[]{:S(2)}, u32[]{:S(2)}) %collective-permute-start.1) | collective-permute-done | bytes 65568 | tf_op jit(solution)/shard_map/ppermute | solution.py:18
  22.0 6.4 %collective-permute-done.2 = bf16[128,256]{0,1:T(8,128)(2,1)S(1)} collective-permute-done((bf16[128,256]{0,1:T(8,128)(2,1)S(1)}, bf16[128,256]{0,1:T(8,128)(2,1)S(1)}, u32[]{:S(2)}, u32[]{:S(2)}) %collective-permute-start.2) | collective-permute-done | bytes 65568 | tf_op jit(solution)/shard_map/ppermute | solution.py:18
  28.4 6.4 %collective-permute-done.3 = bf16[128,256]{0,1:T(8,128)(2,1)S(1)} collective-permute-done((bf16[128,256]{0,1:T(8,128)(2,1)S(1)}, bf16[128,256]{0,1:T(8,128)(2,1)S(1)}, u32[]{:S(2)}, u32[]{:S(2)}) %collective-permute-start.3) | collective-permute-done | bytes 65568 | tf_op jit(solution)/shard_map/ppermute | solution.py:18
  34.8 6.4 %collective-permute-done.4 = bf16[128,256]{0,1:T(8,128)(2,1)S(1)} collective-permute-done((bf16[128,256]{0,1:T(8,128)(2,1)S(1)}, bf16[128,256]{0,1:T(8,128)(2,1)S(1)}, u32[]{:S(2)}, u32[]{:S(2)}) %collective-permute-start.4) | collective-permute-done | bytes 65568 | tf_op jit(solution)/shard_map/ppermute | solution.py:18
  41.2 6.4 %collective-permute-done.5 = bf16[128,256]{0,1:T(8,128)(2,1)S(1)} collective-permute-done((bf16[128,256]{0,1:T(8,128)(2,1)S(1)}, bf16[128,256]{0,1:T(8,128)(2,1)S(1)}, u32[]{:S(2)}, u32[]{:S(2)}) %collective-permute-start.5) | collective-permute-done | bytes 65568 | tf_op jit(solution)/shard_map/ppermute | solution.py:18
  47.6 6.4 %collective-permute-done.6 = bf16[128,256]{0,1:T(8,128)(2,1)S(1)} collective-permute-done((bf16[128,256]{0,1:T(8,128)(2,1)S(1)}, bf16[128,256]{0,1:T(8,128)(2,1)S(1)}, u32[]{:S(2)}, u32[]{:S(2)}) %collective-permute-start.6) | collective-permute-done | bytes 65568 | tf_op jit(solution)/shard_map/ppermute | solution.py:18
  54.0 6.4 %collective-permute-done.7 = bf16[128,256]{0,1:T(8,128)(2,1)S(1)} collective-permute-done((bf16[128,256]{0,1:T(8,128)(2,1)S(1)}, bf16[128,256]{0,1:T(8,128)(2,1)S(1)}, u32[]{:S(2)}, u32[]{:S(2)}) %collective-permute-start.7) | collective-permute-done | bytes 65568 | tf_op jit(solution)/shard_map/ppermute | solution.py:18
  60.4 6.4 %collective-permute-done.8 = bf16[128,256]{0,1:T(8,128)(2,1)S(1)} collective-permute-done((bf16[128,256]{0,1:T(8,128)(2,1)S(1)}, bf16[128,256]{0,1:T(8,128)(2,1)S(1)}, u32[]{:S(2)}, u32[]{:S(2)}) %collective-permute-start.8) | collective-permute-done | bytes 65568 | tf_op jit(solution)/shard_map/ppermute | solution.py:18
  66.8 6.4 %collective-permute-done.9 = bf16[128,256]{0,1:T(8,128)(2,1)S(1)} collective-permute-done((bf16[128,256]{0,1:T(8,128)(2,1)S(1)}, bf16[128,256]{0,1:T(8,128)(2,1)S(1)}, u32[]{:S(2)}, u32[]{:S(2)}) %collective-permute-start.9) | collective-permute-done | bytes 65568 | tf_op jit(solution)/shard_map/ppermute | solution.py:18
  73.1 1.6 %copy.16 = bf16[128,256]{0,1:T(8,128)(2,1)} copy(bf16[128,256]{1,0:T(8,128)(2,1)} %param.8) | data formatting | bytes 131072 | tf_op args[1]
  74.7 4.8 %collective-permute-done.10 = bf16[128,256]{0,1:T(8,128)(2,1)S(1)} collective-permute-done((bf16[128,256]{0,1:T(8,128)(2,1)S(1)}, bf16[128,256]{0,1:T(8,128)(2,1)S(1)}, u32[]{:S(2)}, u32[]{:S(2)}) %collective-permute-start.10) | collective-permute-done | bytes 65568 | tf_op jit(solution)/shard_map/ppermute | solution.py:18
  80.2 5.7 %collective-permute-done.11 = bf16[128,256]{0,1:T(8,128)(2,1)S(1)} collective-permute-done((bf16[128,256]{0,1:T(8,128)(2,1)S(1)}, bf16[128,256]{0,1:T(8,128)(2,1)S(1)}, u32[]{:S(2)}, u32[]{:S(2)}) %collective-permute-start.11) | collective-permute-done | bytes 65568 | tf_op jit(solution)/shard_map/ppermute | solution.py:18
  86.1 1.3 copy.17
  87.7 4.8 %collective-permute-done.12 = bf16[128,256]{0,1:T(8,128)(2,1)S(1)} collective-permute-done((bf16[128,256]{0,1:T(8,128)(2,1)S(1)}, bf16[128,256]{0,1:T(8,128)(2,1)S(1)}, u32[]{:S(2)}, u32[]{:S(2)}) %collective-permute-start.12) | collective-permute-done | bytes 65568 | tf_op jit(solution)/shard_map/ppermute | solution.py:18
  92.5 6.4 %collective-permute-done.13 = bf16[128,256]{0,1:T(8,128)(2,1)S(1)} collective-permute-done((bf16[128,256]{0,1:T(8,128)(2,1)S(1)}, bf16[128,256]{0,1:T(8,128)(2,1)S(1)}, u32[]{:S(2)}, u32[]{:S(2)}) %collective-permute-start.13) | collective-permute-done | bytes 65568 | tf_op jit(solution)/shard_map/ppermute | solution.py:18
  98.9 6.5 %collective-permute-done.14 = bf16[128,256]{0,1:T(8,128)(2,1)S(1)} collective-permute-done((bf16[128,256]{0,1:T(8,128)(2,1)S(1)}, bf16[128,256]{0,1:T(8,128)(2,1)S(1)}, u32[]{:S(2)}, u32[]{:S(2)}) %collective-permute-start.14) | collective-permute-done | bytes 65568 | tf_op jit(solution)/shard_map/ppermute | solution.py:18
  106.3 7.2 %all-gather.2.cloned.1.call-done = bf16[2048,256]{0,1:T(8,128)(2,1)} async-done(((bf16[128,256]{0,1:T(8,128)(2,1)}), bf16[2048,256]{0,1:T(8,128)(2,1)}) %all-gather.2.cloned.1.call-update) | async-done | bytes 1048592 | tf_op jit(solution)/shard_map/all_gather | solution.py:110
  113.5 20.4 %while.20 = (s32[]{:T(128)}, f32[2,7,128]{2,1,0:T(8,128)S(1)}, f32[2,7,128]{2,1,0:T(8,128)S(1)}, f32[2,7,128,128]{3,2,1,0:T(8,128)S(1)}, f32[32,512]{1,0:T(8,128...) while((s32[]{:T(128)}, f32[2,7,128]{2,1,0:T(8,128)S(1)}, ...), condition=%wide.region_3.4_spmd.clone, body=%wide.region_0.3_spmd.clone.sunk | while | flops 499344320 | bytes 16182928 | solution.py:124
  113.8 1.0 constant_dynamic-slice_fusion.4
  116.1 0.9 fusion.48
  117.1 1.5 %fusion.50 = f32[2,7,128,128]{3,2,1,0:T(8,128)S(1)} fusion(bf16[512,2,128,1]{0,2,3,1:T(8,128)(2,1)S(1)} %bitcast.80, f32[2,512,128,7]{2,1,3,0:T(8,128)S(1)} %get-tuple-element.372, f32[2,7,128]{2,1,0:T(8,128)S(1)} %select_maximum_fusion.2, pred[128,512]{0,1:T(8,128)(4,1)S(1)} %broadcast_compare_fusion.2, ...), kind=kOutput, calls=%fused_computation.8.clone.1 | convolution fusion | flops 240156672 | bytes 5847041 | tf_op jit(solution)/shard_map/while/body/eval_jaxpr/hgqk,khd->hgqd/dot_general | solution.py:95
  118.9 1.0 constant_dynamic-slice_fusion.4
  121.2 0.9 fusion.48
  122.1 1.5 %fusion.50 = f32[2,7,128,128]{3,2,1,0:T(8,128)S(1)} fusion(bf16[512,2,128,1]{0,2,3,1:T(8,128)(2,1)S(1)} %bitcast.80, f32[2,512,128,7]{2,1,3,0:T(8,128)S(1)} %get-tuple-element.372, f32[2,7,128]{2,1,0:T(8,128)S(1)} %select_maximum_fusion.2, pred[128,512]{0,1:T(8,128)(4,1)S(1)} %broadcast_compare_fusion.2, ...), kind=kOutput, calls=%fused_computation.8.clone.1 | convolution fusion | flops 240156672 | bytes 5847041 | tf_op jit(solution)/shard_map/while/body/eval_jaxpr/hgqk,khd->hgqd/dot_general | solution.py:95
  124.0 1.0 constant_dynamic-slice_fusion.4
  126.3 0.9 fusion.48
  127.2 1.5 %fusion.50 = f32[2,7,128,128]{3,2,1,0:T(8,128)S(1)} fusion(bf16[512,2,128,1]{0,2,3,1:T(8,128)(2,1)S(1)} %bitcast.80, f32[2,512,128,7]{2,1,3,0:T(8,128)S(1)} %get-tuple-element.372, f32[2,7,128]{2,1,0:T(8,128)S(1)} %select_maximum_fusion.2, pred[128,512]{0,1:T(8,128)(4,1)S(1)} %broadcast_compare_fusion.2, ...), kind=kOutput, calls=%fused_computation.8.clone.1 | convolution fusion | flops 240156672 | bytes 5847041 | tf_op jit(solution)/shard_map/while/body/eval_jaxpr/hgqk,khd->hgqd/dot_general | solution.py:95
  129.1 1.0 constant_dynamic-slice_fusion.4
  132.3 1.5 %fusion.50 = f32[2,7,128,128]{3,2,1,0:T(8,128)S(1)} fusion(bf16[512,2,128,1]{0,2,3,1:T(8,128)(2,1)S(1)} %bitcast.80, f32[2,512,128,7]{2,1,3,0:T(8,128)S(1)} %get-tuple-element.372, f32[2,7,128]{2,1,0:T(8,128)S(1)} %select_maximum_fusion.2, pred[128,512]{0,1:T(8,128)(4,1)S(1)} %broadcast_compare_fusion.2, ...), kind=kOutput, calls=%fused_computation.8.clone.1 | convolution fusion | flops 240156672 | bytes 5847041 | tf_op jit(solution)/shard_map/while/body/eval_jaxpr/hgqk,khd->hgqd/dot_general | solution.py:95
  134.3 1.0 copy.23
  (115 shorter events, 10.7 us)
Async XLA Ops:
  7.2 106.4 %all-gather.2.cloned.1.call-start = ((), (), s32[]{:S(2)}) async-start(), calls=%async_computation | async-start | bytes 1114112 | tf_op jit(solution)/shard_map/all_gather | solution.py:110
  8.2 7.5 %collective-permute-start = (bf16[128,256]{0,1:T(8,128)(2,1)S(1)}, bf16[128,256]{0,1:T(8,128)(2,1)S(1)}, u32[]{:S(2)}, u32[]{:S(2)}) collective-permute-start(bf16[128,256]{0,1:T(8,128)(2,1)S(1)} %copy.18), channel_id=1, source_target_pairs={{0,1},{1,2},{2,3},{3,4},{4,5},{5,6},{6,7},{7,8},{8,9},{9,10},{10,1... | collective-permute-start | bytes 196616 | tf_op jit(solution)/shard_map/ppermute | solution.py:18
  15.6 6.4 %collective-permute-start.1 = (bf16[128,256]{0,1:T(8,128)(2,1)S(1)}, bf16[128,256]{0,1:T(8,128)(2,1)S(1)}, u32[]{:S(2)}, u32[]{:S(2)}) collective-permute-start(bf16[128,256]{0,1:T(8,128)(2,1)S(1)} %collective-permute-done), channel_id=1, source_target_pairs={{0,1},{1,2},{2,3},{3,4},{4,5},{5,6},{6,7},{7,8},{8,9},{9,10},{10,1... | collective-permute-start | bytes 196616 | tf_op jit(solution)/shard_map/ppermute | solution.py:18
  22.0 6.4 %collective-permute-start.2 = (bf16[128,256]{0,1:T(8,128)(2,1)S(1)}, bf16[128,256]{0,1:T(8,128)(2,1)S(1)}, u32[]{:S(2)}, u32[]{:S(2)}) collective-permute-start(bf16[128,256]{0,1:T(8,128)(2,1)S(1)} %collective-permute-done.1), channel_id=1, source_target_pairs={{0,1},{1,2},{2,3},{3,4},{4,5},{5,6},{6,7},{7,8},{8,9},{9,10},{10,1... | collective-permute-start | bytes 196616 | tf_op jit(solution)/shard_map/ppermute | solution.py:18
  28.4 6.4 %collective-permute-start.3 = (bf16[128,256]{0,1:T(8,128)(2,1)S(1)}, bf16[128,256]{0,1:T(8,128)(2,1)S(1)}, u32[]{:S(2)}, u32[]{:S(2)}) collective-permute-start(bf16[128,256]{0,1:T(8,128)(2,1)S(1)} %collective-permute-done.2), channel_id=1, source_target_pairs={{0,1},{1,2},{2,3},{3,4},{4,5},{5,6},{6,7},{7,8},{8,9},{9,10},{10,1... | collective-permute-start | bytes 196616 | tf_op jit(solution)/shard_map/ppermute | solution.py:18
  34.8 6.4 %collective-permute-start.4 = (bf16[128,256]{0,1:T(8,128)(2,1)S(1)}, bf16[128,256]{0,1:T(8,128)(2,1)S(1)}, u32[]{:S(2)}, u32[]{:S(2)}) collective-permute-start(bf16[128,256]{0,1:T(8,128)(2,1)S(1)} %collective-permute-done.3), channel_id=1, source_target_pairs={{0,1},{1,2},{2,3},{3,4},{4,5},{5,6},{6,7},{7,8},{8,9},{9,10},{10,1... | collective-permute-start | bytes 196616 | tf_op jit(solution)/shard_map/ppermute | solution.py:18
  41.2 6.4 %collective-permute-start.5 = (bf16[128,256]{0,1:T(8,128)(2,1)S(1)}, bf16[128,256]{0,1:T(8,128)(2,1)S(1)}, u32[]{:S(2)}, u32[]{:S(2)}) collective-permute-start(bf16[128,256]{0,1:T(8,128)(2,1)S(1)} %collective-permute-done.4), channel_id=1, source_target_pairs={{0,1},{1,2},{2,3},{3,4},{4,5},{5,6},{6,7},{7,8},{8,9},{9,10},{10,1... | collective-permute-start | bytes 196616 | tf_op jit(solution)/shard_map/ppermute | solution.py:18
  47.6 6.4 %collective-permute-start.6 = (bf16[128,256]{0,1:T(8,128)(2,1)S(1)}, bf16[128,256]{0,1:T(8,128)(2,1)S(1)}, u32[]{:S(2)}, u32[]{:S(2)}) collective-permute-start(bf16[128,256]{0,1:T(8,128)(2,1)S(1)} %collective-permute-done.5), channel_id=1, source_target_pairs={{0,1},{1,2},{2,3},{3,4},{4,5},{5,6},{6,7},{7,8},{8,9},{9,10},{10,1... | collective-permute-start | bytes 196616 | tf_op jit(solution)/shard_map/ppermute | solution.py:18
  54.0 6.4 %collective-permute-start.7 = (bf16[128,256]{0,1:T(8,128)(2,1)S(1)}, bf16[128,256]{0,1:T(8,128)(2,1)S(1)}, u32[]{:S(2)}, u32[]{:S(2)}) collective-permute-start(bf16[128,256]{0,1:T(8,128)(2,1)S(1)} %collective-permute-done.6), channel_id=1, source_target_pairs={{0,1},{1,2},{2,3},{3,4},{4,5},{5,6},{6,7},{7,8},{8,9},{9,10},{10,1... | collective-permute-start | bytes 196616 | tf_op jit(solution)/shard_map/ppermute | solution.py:18
  60.4 6.4 %collective-permute-start.8 = (bf16[128,256]{0,1:T(8,128)(2,1)S(1)}, bf16[128,256]{0,1:T(8,128)(2,1)S(1)}, u32[]{:S(2)}, u32[]{:S(2)}) collective-permute-start(bf16[128,256]{0,1:T(8,128)(2,1)S(1)} %collective-permute-done.7), channel_id=1, source_target_pairs={{0,1},{1,2},{2,3},{3,4},{4,5},{5,6},{6,7},{7,8},{8,9},{9,10},{10,1... | collective-permute-start | bytes 196616 | tf_op jit(solution)/shard_map/ppermute | solution.py:18
  66.7 6.4 %collective-permute-start.9 = (bf16[128,256]{0,1:T(8,128)(2,1)S(1)}, bf16[128,256]{0,1:T(8,128)(2,1)S(1)}, u32[]{:S(2)}, u32[]{:S(2)}) collective-permute-start(bf16[128,256]{0,1:T(8,128)(2,1)S(1)} %collective-permute-done.8), channel_id=1, source_target_pairs={{0,1},{1,2},{2,3},{3,4},{4,5},{5,6},{6,7},{7,8},{8,9},{9,10},{10,1... | collective-permute-start | bytes 196616 | tf_op jit(solution)/shard_map/ppermute | solution.py:18
  73.1 6.4 %collective-permute-start.10 = (bf16[128,256]{0,1:T(8,128)(2,1)S(1)}, bf16[128,256]{0,1:T(8,128)(2,1)S(1)}, u32[]{:S(2)}, u32[]{:S(2)}) collective-permute-start(bf16[128,256]{0,1:T(8,128)(2,1)S(1)} %collective-permute-done.9), channel_id=1, source_target_pairs={{0,1},{1,2},{2,3},{3,4},{4,5},{5,6},{6,7},{7,8},{8,9},{9,10},{10,1... | collective-permute-start | bytes 196616 | tf_op jit(solution)/shard_map/ppermute | solution.py:18
  79.5 6.4 %collective-permute-start.11 = (bf16[128,256]{0,1:T(8,128)(2,1)S(1)}, bf16[128,256]{0,1:T(8,128)(2,1)S(1)}, u32[]{:S(2)}, u32[]{:S(2)}) collective-permute-start(bf16[128,256]{0,1:T(8,128)(2,1)S(1)} %collective-permute-done.10), channel_id=1, source_target_pairs={{0,1},{1,2},{2,3},{3,4},{4,5},{5,6},{6,7},{7,8},{8,9},{9,10},{10,1... | collective-permute-start | bytes 196616 | tf_op jit(solution)/shard_map/ppermute | solution.py:18
  85.9 6.6 %collective-permute-start.12 = (bf16[128,256]{0,1:T(8,128)(2,1)S(1)}, bf16[128,256]{0,1:T(8,128)(2,1)S(1)}, u32[]{:S(2)}, u32[]{:S(2)}) collective-permute-start(bf16[128,256]{0,1:T(8,128)(2,1)S(1)} %collective-permute-done.11), channel_id=1, source_target_pairs={{0,1},{1,2},{2,3},{3,4},{4,5},{5,6},{6,7},{7,8},{8,9},{9,10},{10,1... | collective-permute-start | bytes 196616 | tf_op jit(solution)/shard_map/ppermute | solution.py:18
  92.5 6.4 %collective-permute-start.13 = (bf16[128,256]{0,1:T(8,128)(2,1)S(1)}, bf16[128,256]{0,1:T(8,128)(2,1)S(1)}, u32[]{:S(2)}, u32[]{:S(2)}) collective-permute-start(bf16[128,256]{0,1:T(8,128)(2,1)S(1)} %collective-permute-done.12), channel_id=1, source_target_pairs={{0,1},{1,2},{2,3},{3,4},{4,5},{5,6},{6,7},{7,8},{8,9},{9,10},{10,1... | collective-permute-start | bytes 196616 | tf_op jit(solution)/shard_map/ppermute | solution.py:18
  98.9 6.5 %collective-permute-start.14 = (bf16[128,256]{0,1:T(8,128)(2,1)S(1)}, bf16[128,256]{0,1:T(8,128)(2,1)S(1)}, u32[]{:S(2)}, u32[]{:S(2)}) collective-permute-start(bf16[128,256]{0,1:T(8,128)(2,1)S(1)} %collective-permute-done.13), channel_id=1, source_target_pairs={{0,1},{1,2},{2,3},{3,4},{4,5},{5,6},{6,7},{7,8},{8,9},{9,10},{10,1... | collective-permute-start | bytes 196616 | tf_op jit(solution)/shard_map/ppermute | solution.py:18
  105.7 7.8 %copy-start = (s32[2,1]{0,1:T(1,128)S(1)}, s32[2,1]{0,1:T(1,128)}, u32[]{:S(2)}) copy-start(s32[2,1]{0,1:T(1,128)} %param.11) | copy-start | bytes 28
Sparse Core Ops, SparseCore 0:
  74.9 38.6 all-gather.1
